TPU v7x, 32 devices: a whole 2x2x4 slice. The times are simulated.
32 devices in a mesh: band: 16 (over z, y, core), sub: 2 (over x).
Axes of the slice: x: 2, y: 2, z: 4, core: 2. Of those that a mesh axis runs over, the one named last changes fastest.
Arguments:
- land_values: bfloat16 [64, 524288], P(None, ('band', 'sub')), may hold values from -6 to 6
- area_weights: bfloat16 [4096, 128, 128], P(('band', 'sub')), may hold values from 0.0019989014 to 0.029907227
- land_mask: int32 [524288], P(('band', 'sub')), may hold values 0 or 1
- dest_band: int32 [4096, 1], P(('band', 'sub')), may hold values from 0 to 15; in each aligned block of 128 rows (0 to 127, 128 to 255, ...) at most 16 rows name the same one
- dest_tile: int32 [4096], P(('band', 'sub')), may hold values from 0 to 399
- ocean_mask: int32 [819200], P(('band', 'sub')), may hold values 0 or 1
Outputs:
- remapped: float32 [64, 819200], P(None, ('band', 'sub'))
Inputs may be any that keep to these rules, and one draw needn't show every extreme that they name: `dest_band`: each device's 128 blocks name any one band at most 16 times; in every draw some device names one band exactly 16 times.
All inputs are finite; a program needn't handle non-finite values. No bound on the sum of `land_mask` or of `ocean_mask` on one device may be relied on, other than what follows from the above.
Results may differ from a plain program's by a relative error of at most 0.005.
Values may be sent and summed in bfloat16 or wider, within the bound.
A program may use at most 128 MiB of HBM per device.

v0:
```python
import jax
import jax.numpy as jnp
from jax import lax
from jax.sharding import PartitionSpec as P

cover_floor = 0.5


def slot_table(group_key, slot_count, capacity):
    block_order = jnp.arange(group_key.shape[0], dtype=jnp.int32)
    earlier = (group_key[:, None] == group_key[None, :]) & (
        block_order[None, :] < block_order[:, None]
    )
    rank_in = jnp.sum(earlier.astype(jnp.int32), axis=1)
    slot_of = group_key * capacity + rank_in
    return jnp.arange(slot_count, dtype=jnp.int32)[:, None] == slot_of[None, :]


def place_tiles(partial_value, covered, tile_recv, tile_count):
    placing = (tile_recv[:, None] == jnp.arange(tile_count, dtype=jnp.int32)[None, :]).astype(
        jnp.bfloat16
    )
    summed = jnp.einsum("st,sfo->fto", placing, partial_value, preferred_element_type=jnp.float32)
    coverage = jnp.einsum("st,so->to", placing, covered, preferred_element_type=jnp.float32)
    return (summed, coverage)


def per_device(land_values, area_weights, land_mask, dest_band, dest_tile, ocean_mask):
    fields = land_values.shape[0]
    blocks_here = area_weights.shape[0]
    block_cells = area_weights.shape[1]
    tile_cells = area_weights.shape[2]
    band_count = lax.axis_size("band")
    halves = lax.axis_size("sub")
    capacity = max(2, 2 * blocks_here // band_count)
    slot_count = band_count * capacity
    tiles_half = ocean_mask.shape[0] // tile_cells
    tiles_band = tiles_half * halves
    values = land_values.reshape(fields, blocks_here, block_cells)
    masked = (
        area_weights * land_mask.reshape(blocks_here, block_cells).astype(jnp.bfloat16)[:, :, None]
    )
    target = dest_band[:, 0]
    ocean_keep = ocean_mask.reshape(tiles_half, tile_cells).astype(jnp.float32)
    packing = slot_table(target, slot_count, capacity)
    pack_half = packing.astype(jnp.bfloat16)
    tile_sent = jnp.sum(packing.astype(jnp.int32) * dest_tile[None, :], axis=1).reshape(
        band_count, capacity
    )
    partial_local = jnp.einsum(
        "fbl,blo->bfo", values, masked, preferred_element_type=jnp.float32
    ).astype(jnp.bfloat16)
    covered_local = jnp.sum(masked.astype(jnp.float32), axis=1).astype(jnp.bfloat16)
    sent_partial = jnp.einsum(
        "sb,bfo->sfo", pack_half, partial_local, preferred_element_type=jnp.float32
    ).astype(jnp.bfloat16)
    sent_partial = sent_partial.reshape(band_count, capacity, fields, tile_cells)
    sent_covered = jnp.einsum(
        "sb,bo->so", pack_half, covered_local, preferred_element_type=jnp.float32
    ).astype(jnp.bfloat16)
    sent_covered = sent_covered.reshape(band_count, capacity, tile_cells)
    partial_value, covered, tile_recv = (
        lax.all_to_all(sent_partial, "band", split_axis=0, concat_axis=0, tiled=True),
        lax.all_to_all(sent_covered, "band", split_axis=0, concat_axis=0, tiled=True),
        lax.all_to_all(tile_sent, "band", split_axis=0, concat_axis=0, tiled=True),
    )
    summed, coverage = place_tiles(
        partial_value.reshape(slot_count, fields, tile_cells),
        covered.reshape(slot_count, tile_cells),
        tile_recv.reshape(slot_count),
        tiles_band,
    )
    summed, coverage = (
        lax.psum_scatter(summed, "sub", scatter_dimension=1, tiled=True),
        lax.psum_scatter(coverage, "sub", scatter_dimension=0, tiled=True),
    )
    remapped = summed * ocean_keep[None] / jnp.maximum(coverage, cover_floor)[None]
    return remapped.reshape(fields, tiles_half * tile_cells)


def solution(mesh):
    in_specs = (
        P(None, ("band", "sub")),
        P(("band", "sub"), None, None),
        P(("band", "sub")),
        P(("band", "sub"), None),
        P(("band", "sub")),
        P(("band", "sub")),
    )
    out_specs = P(None, ("band", "sub"))
    return jax.shard_map(
        per_device, mesh=mesh, in_specs=in_specs, out_specs=out_specs, check_vma=False
    )
```

profile of v0, /device:TPU:0, one launch (start us, length us, event | category | flops | bytes accessed | tf_op | source)
XLA Modules:
  0.0 313.6 jit_solution(2422943807315207956)
XLA Ops:
  6.5 1.0 convert_reduce_fusion
  7.5 0.7 multiply_add_fusion
  8.2 0.8 select_reduce_fusion
  9.0 0.7 all_to_all.13
  9.7 7.4 %all-to-all-start.1 = ((s32[16,1,16]{2,1,0:T(1,128)}), s32[16,1,16]{2,1,0:T(1,128)S(1)}, u32[]{:S(2)}, u32[]{:S(2)}) async-start(s32[16,1,16]{2,1,0:T(1,128)} %all_to_all.13), calls=%async_computation.1 | async-start | bytes 16384 | tf_op jit(solution)/shard_map/all_to_all | solution.py:65
  17.1 0.0 copy-start.1
  17.1 1.0 convert_bitcast_fusion.2
  18.1 4.7 %multiply_reduce_fusion = bf16[128,128]{1,0:T(8,128)(2,1)S(1)} fusion(bf16[128,128,128]{2,1,0:T(8,128)(2,1)} %param.7, bf16[128,128]{1,0:T(8,128)(2,1)S(1)} %convert_bitcast_fusion.2), kind=kLoop, calls=%fused_computation.3 | loop fusion | flops 4177920 | bytes 4259840 | tf_op jit(solution)/shard_map/reduce_sum | solution.py:53
  22.8 4.1 %convert_bitcast_fusion = bf16[128,64,128]{2,1,0:T(8,128)(2,1)} fusion(bf16[128,128,128]{2,1,0:T(8,128)(2,1)S(1)} %copy-done.1, bf16[128,128]{1,0:T(8,128)(2,1)S(1)} %convert_bitcast_fusion.2, bf16[64,16384]{1,0:T(8,128)(2,1)S(1)} %copy-done), kind=kOutput, calls=%fused_computation.10 | convolution fusion | flops 277872640 | bytes 8421376 | tf_op jit(solution)/shard_map/fbl,blo->bfo/dot_general | solution.py:50
  26.9 0.8 convolution_convert_fusion.1
  27.7 6.0 %all-to-all-start.2 = ((bf16[16,16,128]{2,1,0:T(8,128)(2,1)}), bf16[16,16,128]{2,1,0:T(8,128)(2,1)S(1)}, u32[]{:S(2)}, u32[]{:S(2)}) async-start(bf16[16,16,128]{2,1,0:T(8,128)(2,1)} %bitcast.9), calls=%async_computation.3 | async-start | bytes 131072 | tf_op jit(solution)/shard_map/all_to_all | solution.py:64
  33.7 3.7 %convolution_convert_fusion = bf16[256,64,128]{2,0,1:T(8,128)(2,1)S(1)} fusion(bf16[128,64,128]{2,1,0:T(8,128)(2,1)} %convert_bitcast_fusion, s32[128]{0:T(128)S(1)} %multiply_add_fusion), kind=kOutput, calls=%fused_computation.6 | convolution fusion | flops 539000832 | bytes 6291968 | tf_op jit(solution)/shard_map/sb,bfo->sfo/dot_general | solution.py:54
  37.4 3.1 copy.11
  40.5 0.1 all-to-all-done.2
  40.6 6.0 %all-to-all-start = ((bf16[16,16,64,128]{3,1,2,0:T(8,128)(2,1)}), bf16[16,16,64,128]{3,1,2,0:T(8,128)(2,1)}, u32[]{:S(2)}, u32[]{:S(2)}) async-start(bf16[16,16,64,128]{3,1,2,0:T(8,128)(2,1)} %copy.11), calls=%async_computation | async-start | bytes 8388608 | tf_op jit(solution)/shard_map/all_to_all | solution.py:63
  46.6 0.0 reduce-scatter.7.cloned.1.call-start
  46.6 0.5 broadcast.14
  47.1 0.6 reduce.4
  47.8 0.1 eq.47
  47.9 0.9 fusion.10
  48.8 0.0 reduce-scatter.7.cloned.1.call-update
  48.8 0.0 reduce-scatter.5.cloned.1.call-start
  48.8 75.3 %all-to-all-done = bf16[16,16,64,128]{3,1,2,0:T(8,128)(2,1)} async-done(((bf16[16,16,64,128]{3,1,2,0:T(8,128)(2,1)}), bf16[16,16,64,128]{3,1,2,0:T(8,128)(2,1)}, u32[]{:S(2)}, u32[]{:S(2)}) %all-to-all-start) | async-done | bytes 4194336 | tf_op jit(solution)/shard_map/all_to_all | solution.py:63
  124.1 3.4 %copy.12 = bf16[16,16,64,128]{3,1,0,2:T(8,128)(2,1)S(1)} copy(bf16[16,16,64,128]{3,1,2,0:T(8,128)(2,1)} %all-to-all-done) | data formatting | bytes 8388608 | tf_op jit(solution)/shard_map/all_to_all | solution.py:63
  127.5 6.6 %convolution_bitcast_fusion = f32[64,400,128]{2,1,0:T(8,128)} fusion(bf16[256,64,128]{2,0,1:T(8,128)(2,1)S(1)} %bitcast.38, s32[256]{0:T(256)S(1)} %eq.47), kind=kOutput, calls=%fused_computation | convolution fusion | flops 1677824000 | bytes 17302528 | tf_op jit(solution)/shard_map/st,sfo->fto/dot_general | solution.py:23
  134.1 0.0 reduce-scatter.5.cloned.1.call-update
  134.1 0.9 copy-done.2
  135.0 0.0 reduce-scatter.7.cloned.1.call-done
  135.0 0.9 broadcast_maximum_fusion
  135.9 163.5 %reduce-scatter.5.cloned.1.call-done = f32[64,200,128]{2,1,0:T(8,128)} async-done(((f32[64,400,128]{2,1,0:T(8,128)}), f32[64,200,128]{2,1,0:T(8,128)}) %reduce-scatter.5.cloned.1.call-update) | async-done | bytes 6553616 | tf_op jit(solution)/shard_map/reduce_scatter | solution.py:74
  299.4 3.4 %multiply_divide_fusion = f32[64,200,128]{2,1,0:T(8,128)S(1)} fusion(f32[64,200,128]{2,1,0:T(8,128)} %reduce-scatter.5.cloned.1.call-done, f32[200,128]{1,0:T(8,128)S(1)} %broadcast_maximum_fusion, f32[200,128]{1,0:T(8,128)S(1)} %convert_bitcast_fusion.1), kind=kLoop, calls=%fused_computation.2 | loop fusion | flops 3276800 | bytes 13312000 | tf_op jit(solution)/shard_map/div | solution.py:77
  302.8 4.0 %copy.24 = f32[8,8,200,128]{3,1,2,0:T(8,128)} copy(f32[8,8,200,128]{3,2,1,0:T(8,128)S(1)} %bitcast.37) | data formatting | bytes 13107200
  (6 shorter events, 0.0 us)
Async XLA Ops:
  6.5 16.2 %copy-start = (bf16[64,16384]{1,0:T(8,128)(2,1)S(1)}, bf16[64,16384]{1,0:T(8,128)(2,1)}, u32[]{:S(2)}) copy-start(bf16[64,16384]{1,0:T(8,128)(2,1)} %param.6) | copy-start | bytes 6291460
  9.7 18.0 %all-to-all-start.1 = ((s32[16,1,16]{2,1,0:T(1,128)}), s32[16,1,16]{2,1,0:T(1,128)S(1)}, u32[]{:S(2)}, u32[]{:S(2)}) async-start(s32[16,1,16]{2,1,0:T(1,128)} %all_to_all.13), calls=%async_computation.1 | async-start | bytes 16384 | tf_op jit(solution)/shard_map/all_to_all | solution.py:65
  17.1 5.7 %copy-start.1 = (bf16[128,128,128]{2,1,0:T(8,128)(2,1)S(1)}, bf16[128,128,128]{2,1,0:T(8,128)(2,1)}, u32[]{:S(2)}) copy-start(bf16[128,128,128]{2,1,0:T(8,128)(2,1)} %param.7) | copy-start | bytes 12582916
  27.7 12.9 %all-to-all-start.2 = ((bf16[16,16,128]{2,1,0:T(8,128)(2,1)}), bf16[16,16,128]{2,1,0:T(8,128)(2,1)S(1)}, u32[]{:S(2)}, u32[]{:S(2)}) async-start(bf16[16,16,128]{2,1,0:T(8,128)(2,1)} %bitcast.9), calls=%async_computation.3 | async-start | bytes 131072 | tf_op jit(solution)/shard_map/all_to_all | solution.py:64
  40.6 83.5 %all-to-all-start = ((bf16[16,16,64,128]{3,1,2,0:T(8,128)(2,1)}), bf16[16,16,64,128]{3,1,2,0:T(8,128)(2,1)}, u32[]{:S(2)}, u32[]{:S(2)}) async-start(bf16[16,16,64,128]{3,1,2,0:T(8,128)(2,1)} %copy.11), calls=%async_computation | async-start | bytes 8388608 | tf_op jit(solution)/shard_map/all_to_all | solution.py:63
  46.6 88.4 %reduce-scatter.7.cloned.1.call-start = ((), (), s32[]{:S(2)}) async-start(), calls=%async_computation.6 | async-start | bytes 307200
  48.8 250.6 %reduce-scatter.5.cloned.1.call-start = ((), (), s32[]{:S(2)}) async-start(), calls=%async_computation.5 | async-start | bytes 19660800 | tf_op jit(solution)/shard_map/reduce_scatter | solution.py:74
  134.1 0.9 copy-start.2
Sparse Core Ops, SparseCore 0:
  49.6 12.3 reduce-scatter.6
  134.2 165.1 reduce-scatter.4
where the time goes:
time: 314 us
  waiting for transfers between devices  239 us (76%)
  starting transfers between devices  19.5 us (6%)
  matrix products  16 us (5%)
  between operations  13.5 us (4%)
  other arithmetic  13 us (4%)
  local copies, waits for them, and re-layouts  12.6 us (4%)
    reduce_scatter x1, waiting for transfers between devices, per_device(): lax.psum_scatter(summed, 'sub', scatter_dimension=1, tiled=True)  164 us
    all_to_all x1, waiting for transfers between devices, per_device(): lax.all_to_all(sent_partial, 'band', split_axis=0, concat_axis=0, tiled=T...  75.3 us
    all_to_all x1, starting transfers between devices, per_device(): lax.all_to_all(tile_sent, 'band', split_axis=0, concat_axis=0, tiled=True)  7.41 us
    dot_general x1, matrix products, place_tiles(): jnp.einsum('st,sfo->fto', placing, partial_value, preferred_element_type=...  6.55 us
  transfers between devices with their start and end apart: 5, of which 3 were waited for; matrix products, arithmetic and copies ran while one was open for 10% of the time, Pallas kernels for 0%

commit v1 on v0

v1 whole, which is shorter than its diff:
```python
import functools

import jax
import jax.numpy as jnp
from jax import lax
from jax.experimental import pallas as pl
from jax.experimental.pallas import tpu as pltpu
from jax.sharding import PartitionSpec as P

cover_floor = 0.5
ROWS = 16


def block_kernel(group, chunks, v_ref, w_ref, m_ref, p_ref, c_ref):
    cells = w_ref.shape[1]
    for j in range(group):
        lanes = pl.ds(j * cells, cells)
        m = m_ref[:, lanes].astype(jnp.float32)
        mb = m.astype(jnp.bfloat16)
        lhs = jnp.concatenate(
            [v_ref[:, lanes] * mb, jnp.broadcast_to(mb, (ROWS, cells))], axis=0
        )
        p = jnp.dot(lhs, w_ref[j], preferred_element_type=jnp.float32)
        for c in range(chunks):
            p_ref[c, j] = p[c * ROWS:(c + 1) * ROWS].astype(jnp.bfloat16)
        c_ref[pl.ds(j, 1), :] = (
            p[chunks * ROWS:chunks * ROWS + 1].astype(jnp.bfloat16).astype(jnp.float32)
        )


def block_products(values, weights, mask):
    fields = values.shape[0]
    blocks, cells, out_cells = weights.shape
    chunks = fields // ROWS
    group = 16
    return pl.pallas_call(
        functools.partial(block_kernel, group, chunks),
        grid=(blocks // group,),
        in_specs=[
            pl.BlockSpec((fields, group * cells), lambda i: (0, i)),
            pl.BlockSpec((group, cells, out_cells), lambda i: (i, 0, 0)),
            pl.BlockSpec((1, group * cells), lambda i: (0, i)),
        ],
        out_specs=[
            pl.BlockSpec((chunks, group, ROWS, out_cells), lambda i: (0, i, 0, 0)),
            pl.BlockSpec((group, out_cells), lambda i: (i, 0)),
        ],
        out_shape=[
            jax.ShapeDtypeStruct((chunks, blocks, ROWS, out_cells), jnp.bfloat16),
            jax.ShapeDtypeStruct((blocks, out_cells), jnp.float32),
        ],
        name="block_products",
        cost_estimate=pl.CostEstimate(
            flops=2 * blocks * fields * cells * out_cells,
            bytes_accessed=8 * 1024 * 1024,
            transcendentals=0,
        ),
    )(values, weights, mask)


def exchange_kernel(
    bands, cap, chunks, tiles,
    src_ref, prev_ref, last_ref, p_ref, c_ref, keep_ref, out_ref,
    send, recv, csend, crecv, run, crun, xsend, xrecv, cxsend, cxrecv,
    send_sem, recv_sem, csend_sem, crecv_sem, xsend_sem, xrecv_sem,
):
    me = lax.axis_index("band")
    half = lax.axis_index("sub")
    slots = bands * cap
    other = {"sub": 1 - half}

    barrier = pltpu.get_barrier_semaphore()

    @pl.loop(1, bands)
    def _(k):
        pl.semaphore_signal(
            barrier, inc=1, device_id={"band": lax.rem(me + k, bands)},
            device_id_type=pl.DeviceIdType.MESH,
        )

    pl.semaphore_signal(barrier, inc=1, device_id=other, device_id_type=pl.DeviceIdType.MESH)
    pl.semaphore_wait(barrier, bands)

    def chunk_copy(c, d, source):
        return pltpu.make_async_remote_copy(
            src_ref=send.at[c, d], dst_ref=recv.at[c, source],
            send_sem=send_sem.at[c, d], recv_sem=recv_sem.at[c, source],
            device_id={"band": d}, device_id_type=pl.DeviceIdType.MESH,
        )

    def cover_copy(d, source):
        return pltpu.make_async_remote_copy(
            src_ref=csend.at[d], dst_ref=crecv.at[source],
            send_sem=csend_sem.at[d], recv_sem=crecv_sem.at[source],
            device_id={"band": d}, device_id_type=pl.DeviceIdType.MESH,
        )

    def half_copy(c):
        return pltpu.make_async_remote_copy(
            src_ref=xsend.at[c], dst_ref=xrecv.at[c],
            send_sem=xsend_sem.at[c], recv_sem=xrecv_sem.at[c],
            device_id=other, device_id_type=pl.DeviceIdType.MESH,
        )

    half_cover = pltpu.make_async_remote_copy(
        src_ref=cxsend, dst_ref=cxrecv,
        send_sem=xsend_sem.at[chunks], recv_sem=xrecv_sem.at[chunks],
        device_id=other, device_id_type=pl.DeviceIdType.MESH,
    )

    @pl.loop(1, bands)
    def _(k):
        d = lax.rem(me + k, bands)
        for j in range(cap):
            csend[d, pl.ds(j, 1), :] = c_ref[pl.ds(src_ref[d * cap + j], 1), :]
        cover_copy(d, me).start()

    for j in range(cap):
        crecv[me, pl.ds(j, 1), :] = c_ref[pl.ds(src_ref[me * cap + j], 1), :]

    for c in range(chunks):
        @pl.loop(1, bands)
        def _(k, c=c):
            d = lax.rem(me + k, bands)
            for j in range(cap):
                send[c, d, j] = p_ref[c, src_ref[d * cap + j]]
            chunk_copy(c, d, me).start()

        for j in range(cap):
            recv[c, me, j] = p_ref[c, src_ref[me * cap + j]]

    @pl.loop(1, bands)
    def _(k):
        cover_copy(me, lax.rem(me + k, bands)).wait_recv()

    crun[pl.ds(slots, 8), :] = jnp.zeros((8, crun.shape[1]), jnp.float32)

    @pl.loop(0, bands)
    def _(s):
        for j in range(cap):
            i = s * cap + j
            crun[pl.ds(i, 1), :] = (
                crun[pl.ds(prev_ref[i], 1), :] + crecv[s, pl.ds(j, 1), :]
            )

    step = 8

    @pl.loop(0, tiles // step)
    def _(g):
        for u in range(step):
            t = g * step + u
            cxsend[pl.ds(t, 1), :] = crun[pl.ds(last_ref[t], 1), :]

    half_cover.start()

    for c in range(chunks):
        @pl.loop(1, bands)
        def _(k, c=c):
            chunk_copy(c, me, lax.rem(me + k, bands)).wait_recv()

        run[c, slots] = jnp.zeros(run.shape[2:], jnp.float32)

        @pl.loop(0, bands)
        def _(s, c=c):
            for j in range(cap):
                i = s * cap + j
                run[c, i] = run[c, prev_ref[i]] + recv[c, s, j].astype(jnp.float32)

        @pl.loop(0, tiles // step)
        def _(g, c=c):
            for u in range(step):
                t = g * step + u
                xsend[c, t] = run[c, last_ref[t]].astype(jnp.bfloat16)

        half_copy(c).start()

    half_cover.wait_recv()

    @pl.loop(0, tiles // step)
    def _(g):
        for u in range(step):
            t = g * step + u
            row = pl.ds(t, 1)
            total = crun[pl.ds(last_ref[tiles + t], 1), :] + cxrecv[row, :]
            cxrecv[row, :] = keep_ref[row, :] / jnp.maximum(total, cover_floor)

    cells = xsend.shape[3]
    for c in range(chunks):
        half_copy(c).wait_recv()

        @pl.loop(0, tiles // step)
        def _(g, c=c):
            for u in range(step):
                t = g * step + u
                total = run[c, last_ref[tiles + t]] + xrecv[c, t].astype(jnp.float32)
                lanes = pl.ds(pl.multiple_of(t * cells, cells), cells)
                out_ref[pl.ds(c * ROWS, ROWS), lanes] = total * cxrecv[pl.ds(t, 1), :]

    half_cover.wait_send()
    for c in range(chunks):
        half_copy(c).wait_send()

    @pl.loop(1, bands)
    def _(k):
        d = lax.rem(me + k, bands)
        cover_copy(d, me).wait_send()
        for c in range(chunks):
            chunk_copy(c, d, me).wait_send()


def exchange(bands, cap, src, prev, last, partial, covered, keep):
    chunks, _, rows, cells = partial.shape
    tiles = keep.shape[0]
    slots = bands * cap
    smem = pl.BlockSpec(memory_space=pltpu.SMEM)
    vmem = pl.BlockSpec(memory_space=pltpu.VMEM)
    bf16, f32 = jnp.bfloat16, jnp.float32
    dma = pltpu.SemaphoreType.DMA
    return pl.pallas_call(
        functools.partial(exchange_kernel, bands, cap, chunks, tiles),
        in_specs=[smem, smem, smem, vmem, vmem, vmem],
        out_specs=vmem,
        out_shape=jax.ShapeDtypeStruct((chunks * rows, tiles * cells), f32),
        scratch_shapes=[
            pltpu.VMEM((chunks, bands, cap, rows, cells), bf16),
            pltpu.VMEM((chunks, bands, cap, rows, cells), bf16),
            pltpu.VMEM((bands, cap, cells), f32),
            pltpu.VMEM((bands, cap, cells), f32),
            pltpu.VMEM((chunks, slots + 1, rows, cells), f32),
            pltpu.VMEM((slots + 8, cells), f32),
            pltpu.VMEM((chunks, tiles, rows, cells), bf16),
            pltpu.VMEM((chunks, tiles, rows, cells), bf16),
            pltpu.VMEM((tiles, cells), f32),
            pltpu.VMEM((tiles, cells), f32),
            dma((chunks, bands)),
            dma((chunks, bands)),
            dma((bands,)),
            dma((bands,)),
            dma((chunks + 1,)),
            dma((chunks + 1,)),
        ],
        compiler_params=pltpu.CompilerParams(
            collective_id=0, has_side_effects=True, vmem_limit_bytes=60 * 1024 * 1024
        ),
        name="exchange",
    )(src, prev, last, partial, covered, keep)


def per_device(land_values, area_weights, land_mask, dest_band, dest_tile, ocean_mask):
    blocks_here = area_weights.shape[0]
    tile_cells = area_weights.shape[2]
    bands = lax.axis_size("band")
    halves = lax.axis_size("sub")
    half = lax.axis_index("sub")
    cap = max(2, 2 * blocks_here // bands)
    slots = bands * cap
    tiles = ocean_mask.shape[0] // tile_cells

    target = dest_band[:, 0]
    order = jnp.arange(blocks_here, dtype=jnp.int32)
    earlier = (target[:, None] == target[None, :]) & (order[None, :] < order[:, None])
    slot_of = target * cap + jnp.sum(earlier.astype(jnp.int32), axis=1)
    slot_ids = jnp.arange(slots, dtype=jnp.int32)
    packing = (slot_ids[:, None] == slot_of[None, :]).astype(jnp.int32)
    src = jnp.sum(packing * order[None, :], axis=1)
    tile_sent = jnp.sum(packing * (dest_tile + 1)[None, :], axis=1) - 1
    tile_recv = lax.all_to_all(
        tile_sent.reshape(bands, cap), "band", split_axis=0, concat_axis=0, tiled=True
    ).reshape(slots)

    partial, covered = block_products(land_values, area_weights, land_mask[None, :])

    same = (tile_recv[:, None] == tile_recv[None, :]) & (slot_ids[None, :] < slot_ids[:, None])
    prev = jnp.max(jnp.where(same, slot_ids[None, :], -1), axis=1)
    prev = jnp.where(prev < 0, slots, prev)
    listed = jnp.arange(halves * tiles, dtype=jnp.int32)
    listed = lax.rem(listed + (1 - half) * tiles, halves * tiles)
    hit = listed[:, None] == tile_recv[None, :]
    last = jnp.max(jnp.where(hit, slot_ids[None, :], -1), axis=1)
    last = jnp.where(last < 0, slots, last)

    keep = ocean_mask.reshape(tiles, tile_cells).astype(jnp.float32)
    return exchange(bands, cap, src, prev, last, partial, covered, keep)


def solution(mesh):
    in_specs = (
        P(None, ("band", "sub")),
        P(("band", "sub"), None, None),
        P(("band", "sub")),
        P(("band", "sub"), None),
        P(("band", "sub")),
        P(("band", "sub")),
    )
    out_specs = P(None, ("band", "sub"))
    return jax.shard_map(
        per_device, mesh=mesh, in_specs=in_specs, out_specs=out_specs, check_vma=False
    )
```

time: 314 us -> 166 us (0.53)
  the two profiles are of different devices: /device:TPU:0 before, /device:TPU:13 now
where the time goes in v1:
time: 166 us
  Pallas kernels  146 us (88%)
  local copies, waits for them, and re-layouts  7.48 us (5%)
  starting transfers between devices  6.52 us (4%)
  other arithmetic  6.16 us (4%)
    pallas_call x1, Pallas kernels, exchange(): pl.pallas_call(functools.partial(exchange_kernel, bands, cap, chunks, til...  138 us
    pallas_call x1, Pallas kernels, block_products(): pl.pallas_call(functools.partial(block_kernel, group, chunks), grid=(bloc...  7.55 us
    all_to_all x1, starting transfers between devices, per_device(): lax.all_to_all(tile_sent.reshape(bands, cap), 'band', split_axis=0, conca...  6.52 us
    unnamed x1, local copies, waits for them, and re-layouts  6.12 us
  transfers between devices with their start and end apart: 1, of which 0 were waited for; matrix products, arithmetic and copies ran while one was open for 1% of the time, Pallas kernels for 5%

profile of v1, /device:TPU:13, one launch (start us, length us, event | category | flops | bytes accessed | tf_op | source)
XLA Modules:
  0.0 165.8 jit_solution(1076835494153000387)
XLA Ops:
  0.0 0.9 convert_reduce_fusion
  0.9 0.7 multiply_add_fusion
  1.6 0.7 select_reduce_fusion.2
  2.3 0.7 sub.10
  3.0 6.5 %all-to-all-start = ((s32[16,1,16]{2,1,0:T(1,128)}), s32[16,1,16]{2,1,0:T(1,128)S(1)}, u32[]{:S(2)}, u32[]{:S(2)}) async-start(s32[16,1,16]{2,1,0:T(1,128)} %sub.10), calls=%async_computation | async-start | bytes 16384 | tf_op jit(solution)/shard_map/all_to_all | solution.py:267
  9.5 1.5 convert_bitcast_fusion.keep_ref
  11.1 7.6 %block_products.1 = (bf16[4,128,16,128]{3,2,1,0:T(8,128)(2,1)}, f32[128,128]{1,0:T(8,128)}) custom-call(bf16[64,16384]{1,0:T(8,128)(2,1)} %v_ref.1, bf16[128,128,128]{2,1,0:T(8,128)(2,1)} %w_ref.1, s32[1,16384]{1,0:T(1,128)} %bitcast.5), custom_call_target="tpu_custom_call" | custom-call | flops 268435456 | bytes 8388608 | tf_op jit(solution)/shard_map/block_products/pallas_call | solution.py:36
  18.6 0.0 all-to-all-done
  18.6 0.6 broadcast.38
  19.2 0.7 reduce.3
  19.9 0.1 eq.60
  20.0 0.2 select_reduce_fusion.1
  20.2 0.2 select_reduce_fusion
  20.4 0.6 compare_select_fusion.1.prev_ref
  21.0 0.6 compare_select_fusion.last_ref
  21.6 138.1 %exchange.1 = f32[64,25600]{1,0:T(8,128)} custom-call(s32[256]{0:T(256)} %get-tuple-element.10.src_ref, s32[256]{0:T(256)} %compare_select_fusion.1.prev_ref, s32[400]{0:T(512)} %compare_select_fusion.last_ref, bf16[4,128,16,128]{3,2,1,0:T(8,128)(2,1)} %get-tuple-element.7.p_ref, f32[128,128]{1,0:T(8,128)} %get-tuple-element.8.c_ref, ...), custom_call_target="tpu_custom_call" | custom-call | tf_op jit(solution)/shard_map/exchange/pallas_call | solution.py:219
  159.7 6.1 %copy.8 = f32[64,25600]{1,0:T(8,128)} copy(f32[64,25600]{1,0:T(8,128)} %exchange.1) | data formatting | bytes 13107200
  (2 shorter events, 0.0 us)
Async XLA Ops:
  3.0 15.6 %all-to-all-start = ((s32[16,1,16]{2,1,0:T(1,128)}), s32[16,1,16]{2,1,0:T(1,128)S(1)}, u32[]{:S(2)}, u32[]{:S(2)}) async-start(s32[16,1,16]{2,1,0:T(1,128)} %sub.10), calls=%async_computation | async-start | bytes 16384 | tf_op jit(solution)/shard_map/all_to_all | solution.py:267

commit v2 on v1

v2 whole, which is shorter than its diff:
```python
import functools

import jax
import jax.numpy as jnp
from jax import lax
from jax.experimental import pallas as pl
from jax.experimental.pallas import tpu as pltpu
from jax.sharding import PartitionSpec as P

cover_floor = 0.5
ROWS = 8
LANES = 128
MESH = pl.DeviceIdType.MESH


def target_of(me, k, bands):
    if bands & (bands - 1):
        return lax.rem(me + k, bands)
    peer, bit = 0, 1
    while bit < bands:
        peer = peer + bit * lax.rem(me // bit + k // bit, 2)
        bit *= 2
    return peer


def greet_bands(barrier, me, bands):
    @pl.loop(1, bands)
    def _(k):
        pl.semaphore_signal(
            barrier, inc=1, device_id={"band": target_of(me, k, bands)}, device_id_type=MESH
        )


def block_kernel(
    group, chunks, bands, v_ref, w_ref, m_ref, t_ref, p_ref, c_ref, r_ref,
    landed, send_sem, recv_sem,
):
    me = lax.axis_index("band")
    cells = w_ref.shape[1]

    def index_copy(k):
        d = target_of(me, k, bands)
        return pltpu.make_async_remote_copy(
            src_ref=t_ref.at[d], dst_ref=landed.at[k],
            send_sem=send_sem.at[k], recv_sem=recv_sem.at[k],
            device_id={"band": d}, device_id_type=MESH,
        )

    @pl.when(pl.program_id(0) == 0)
    def _():
        barrier = pltpu.get_barrier_semaphore()
        greet_bands(barrier, me, bands)
        pl.semaphore_wait(barrier, bands - 1)

        @pl.loop(1, bands)
        def _(k):
            index_copy(k).start()

    for j in range(group):
        lanes = pl.ds(j * cells, cells)
        mb = m_ref[:, lanes].astype(jnp.float32).astype(jnp.bfloat16)
        lhs = jnp.concatenate(
            [v_ref[:, lanes] * mb, jnp.broadcast_to(mb, (16, cells))], axis=0
        )
        p = jnp.dot(lhs, w_ref[j], preferred_element_type=jnp.float32)
        for c in range(chunks):
            p_ref[c, j] = p[c * ROWS:(c + 1) * ROWS].astype(jnp.bfloat16)
        c_ref[pl.ds(j, 1), :] = (
            p[chunks * ROWS:chunks * ROWS + 1].astype(jnp.bfloat16).astype(jnp.float32)
        )

    @pl.when(pl.program_id(0) == pl.num_programs(0) - 1)
    def _():
        @pl.loop(1, bands)
        def _(k):
            index_copy(k).wait_send()
            index_copy(k).wait_recv()

        r_ref[0] = t_ref[me]
        r_ref[pl.ds(1, bands - 1)] = landed[pl.ds(1, bands - 1)]


def block_products(bands, values, weights, mask, tile_sent):
    fields = values.shape[0]
    blocks, cells, out_cells = weights.shape
    chunks = fields // ROWS
    group = 16
    return pl.pallas_call(
        functools.partial(block_kernel, group, chunks, bands),
        grid=(blocks // group,),
        in_specs=[
            pl.BlockSpec((fields, group * cells), lambda i: (0, i)),
            pl.BlockSpec((group, cells, out_cells), lambda i: (i, 0, 0)),
            pl.BlockSpec((1, group * cells), lambda i: (0, i)),
            pl.BlockSpec(memory_space=pltpu.VMEM),
        ],
        out_specs=[
            pl.BlockSpec((chunks, group, ROWS, out_cells), lambda i: (0, i, 0, 0)),
            pl.BlockSpec((group, out_cells), lambda i: (i, 0)),
            pl.BlockSpec(memory_space=pltpu.VMEM),
        ],
        out_shape=[
            jax.ShapeDtypeStruct((chunks, blocks, ROWS, out_cells), jnp.bfloat16),
            jax.ShapeDtypeStruct((blocks, out_cells), jnp.float32),
            jax.ShapeDtypeStruct(tile_sent.shape, jnp.int32),
        ],
        scratch_shapes=[
            pltpu.VMEM(tile_sent.shape, jnp.int32),
            pltpu.SemaphoreType.DMA((bands,)),
            pltpu.SemaphoreType.DMA((bands,)),
        ],
        compiler_params=pltpu.CompilerParams(collective_id=1, has_side_effects=True),
        name="block_products",
    )(values, weights, mask, tile_sent)


def exchange_kernel(
    bands, cap, chunks, tiles,
    src_ref, prev_ref, last_ref, p_ref, c_ref, wet_ref, out_ref,
    send, recv, csend, crecv, run, crun, xsend, xrecv, cxsend, cxrecv, done,
    send_sem, recv_sem, csend_sem, crecv_sem, xsend_sem, xrecv_sem, out_sem,
):
    me = lax.axis_index("band")
    half = lax.axis_index("sub")
    slots = bands * cap
    cells = xsend.shape[3]
    other = {"sub": 1 - half}
    step = 8

    barrier = pltpu.get_barrier_semaphore()
    greet_bands(barrier, me, bands)
    pl.semaphore_signal(barrier, inc=1, device_id=other, device_id_type=MESH)
    pl.semaphore_wait(barrier, bands)

    def chunk_copy(c, k):
        return pltpu.make_async_remote_copy(
            src_ref=send.at[c, k], dst_ref=recv.at[c, k],
            send_sem=send_sem.at[c, k], recv_sem=recv_sem.at[c, k],
            device_id={"band": target_of(me, k, bands)}, device_id_type=MESH,
        )

    def cover_copy(k):
        return pltpu.make_async_remote_copy(
            src_ref=csend.at[k], dst_ref=crecv.at[k],
            send_sem=csend_sem.at[k], recv_sem=crecv_sem.at[k],
            device_id={"band": target_of(me, k, bands)}, device_id_type=MESH,
        )

    def half_copy(c):
        return pltpu.make_async_remote_copy(
            src_ref=xsend.at[c], dst_ref=xrecv.at[c],
            send_sem=xsend_sem.at[c], recv_sem=xrecv_sem.at[c],
            device_id=other, device_id_type=MESH,
        )

    half_cover = pltpu.make_async_remote_copy(
        src_ref=cxsend, dst_ref=cxrecv,
        send_sem=xsend_sem.at[chunks], recv_sem=xrecv_sem.at[chunks],
        device_id=other, device_id_type=MESH,
    )

    def out_copy(c):
        return pltpu.make_async_copy(
            done.at[c % 2], out_ref.at[pl.ds(c * ROWS, ROWS), :], out_sem.at[c % 2]
        )

    def each_tile(body):
        @pl.loop(0, tiles // step)
        def _(g):
            for u in range(step):
                body(g * step + u)

    def finish(c):
        half_copy(c).wait_recv()
        if c >= 2:
            out_copy(c - 2).wait()

        def one(t):
            total = run[c, last_ref[tiles + t]] + xrecv[c, t].astype(jnp.float32)
            lanes = pl.ds(pl.multiple_of(t * cells, cells), cells)
            done[c % 2, :, lanes] = total * cxrecv[pl.ds(t, 1), :]

        each_tile(one)
        out_copy(c).start()

    def send_chunk(c):
        @pl.loop(1, bands)
        def _(k):
            d = target_of(me, k, bands)
            for j in range(cap):
                send[c, k, j] = p_ref[c, src_ref[d * cap + j]]
            chunk_copy(c, k).start()

        for j in range(cap):
            recv[c, 0, j] = p_ref[c, src_ref[me * cap + j]]

    send_chunk(0)

    @pl.loop(1, bands)
    def _(k):
        d = target_of(me, k, bands)
        for j in range(cap):
            csend[k, pl.ds(j, 1), :] = c_ref[pl.ds(src_ref[d * cap + j], 1), :]
        cover_copy(k).start()

    for j in range(cap):
        crecv[0, pl.ds(j, 1), :] = c_ref[pl.ds(src_ref[me * cap + j], 1), :]

    for c in range(1, chunks):
        send_chunk(c)

    for c in range(chunks):
        run[c, slots] = jnp.zeros(run.shape[2:], jnp.float32)

        def add(k, c=c):
            for j in range(cap):
                i = k * cap + j
                run[c, i] = run[c, prev_ref[i]] + recv[c, k, j].astype(jnp.float32)

        add(0)

        @pl.loop(1, bands)
        def _(k, c=c):
            chunk_copy(c, k).wait_recv()
            add(k)

        def give(t, c=c):
            xsend[c, t] = run[c, last_ref[t]].astype(jnp.bfloat16)

        each_tile(give)
        half_copy(c).start()

        if c == 0:
            @pl.loop(1, bands)
            def _(k):
                cover_copy(k).wait_recv()

            crun[pl.ds(slots, 8), :] = jnp.zeros((8, cells), jnp.float32)

            @pl.loop(0, bands)
            def _(k):
                for j in range(cap):
                    i = k * cap + j
                    crun[pl.ds(i, 1), :] = (
                        crun[pl.ds(prev_ref[i], 1), :] + crecv[k, pl.ds(j, 1), :]
                    )

            def give_cover(t):
                cxsend[pl.ds(t, 1), :] = crun[pl.ds(last_ref[t], 1), :]

            each_tile(give_cover)
            half_cover.start()

        if c == 1:
            half_cover.wait_recv()

            def factor(t):
                row = pl.ds(t, 1)
                total = crun[pl.ds(last_ref[tiles + t], 1), :] + cxrecv[row, :]
                wet = wet_ref[row, :].astype(jnp.float32)
                cxrecv[row, :] = wet / jnp.maximum(total, cover_floor)

            each_tile(factor)

        if c >= 1:
            finish(c - 1)

    finish(chunks - 1)

    half_cover.wait_send()
    for c in range(chunks):
        half_copy(c).wait_send()

    @pl.loop(1, bands)
    def _(k):
        cover_copy(k).wait_send()
        for c in range(chunks):
            chunk_copy(c, k).wait_send()

    for c in range(max(0, chunks - 2), chunks):
        out_copy(c).wait()


def exchange(bands, cap, src, prev, last, partial, covered, wet):
    chunks, _, rows, cells = partial.shape
    tiles = wet.shape[0]
    slots = bands * cap
    smem = pl.BlockSpec(memory_space=pltpu.SMEM)
    vmem = pl.BlockSpec(memory_space=pltpu.VMEM)
    bf16, f32 = jnp.bfloat16, jnp.float32
    dma = pltpu.SemaphoreType.DMA
    return pl.pallas_call(
        functools.partial(exchange_kernel, bands, cap, chunks, tiles),
        in_specs=[smem, smem, smem, vmem, vmem, vmem],
        out_specs=pl.BlockSpec(memory_space=pl.ANY),
        out_shape=jax.ShapeDtypeStruct((chunks * rows, tiles * cells), f32),
        scratch_shapes=[
            pltpu.VMEM((chunks, bands, cap, rows, cells), bf16),
            pltpu.VMEM((chunks, bands, cap, rows, cells), bf16),
            pltpu.VMEM((bands, cap, cells), f32),
            pltpu.VMEM((bands, cap, cells), f32),
            pltpu.VMEM((chunks, slots + 1, rows, cells), f32),
            pltpu.VMEM((slots + 8, cells), f32),
            pltpu.VMEM((chunks, tiles, rows, cells), bf16),
            pltpu.VMEM((chunks, tiles, rows, cells), bf16),
            pltpu.VMEM((tiles, cells), f32),
            pltpu.VMEM((tiles, cells), f32),
            pltpu.VMEM((2, rows, tiles * cells), f32),
            dma((chunks, bands)),
            dma((chunks, bands)),
            dma((bands,)),
            dma((bands,)),
            dma((chunks + 1,)),
            dma((chunks + 1,)),
            dma((2,)),
        ],
        compiler_params=pltpu.CompilerParams(
            collective_id=0, has_side_effects=True, vmem_limit_bytes=60 * 1024 * 1024
        ),
        name="exchange",
    )(src, prev, last, partial, covered, wet)


def per_device(land_values, area_weights, land_mask, dest_band, dest_tile, ocean_mask):
    blocks_here = area_weights.shape[0]
    tile_cells = area_weights.shape[2]
    bands = lax.axis_size("band")
    halves = lax.axis_size("sub")
    half = lax.axis_index("sub")
    cap = max(2, 2 * blocks_here // bands)
    slots = bands * cap
    tiles = ocean_mask.shape[0] // tile_cells

    target = dest_band[:, 0]
    order = jnp.arange(blocks_here, dtype=jnp.int32)
    earlier = (target[:, None] == target[None, :]) & (order[None, :] < order[:, None])
    slot_of = target * cap + jnp.sum(earlier.astype(jnp.int32), axis=1)
    slot_ids = jnp.arange(slots, dtype=jnp.int32)
    packing = (slot_ids[:, None] == slot_of[None, :]).astype(jnp.int32)
    src = jnp.sum(packing * order[None, :], axis=1)
    tile_sent = jnp.sum(packing * (dest_tile + 1)[None, :], axis=1) - 1
    tile_sent = jnp.pad(
        tile_sent.reshape(bands, 1, cap), ((0, 0), (0, 0), (0, LANES - cap)), constant_values=-1
    )

    partial, covered, tile_recv = block_products(
        bands, land_values, area_weights, land_mask[None, :], tile_sent
    )
    tile_recv = tile_recv[:, 0, :cap].reshape(slots)

    same = (tile_recv[:, None] == tile_recv[None, :]) & (slot_ids[None, :] < slot_ids[:, None])
    prev = jnp.max(jnp.where(same, slot_ids[None, :], -1), axis=1)
    prev = jnp.where(prev < 0, slots, prev)
    listed = jnp.arange(halves * tiles, dtype=jnp.int32)
    listed = lax.rem(listed + (1 - half) * tiles, halves * tiles)
    hit = listed[:, None] == tile_recv[None, :]
    last = jnp.max(jnp.where(hit, slot_ids[None, :], -1), axis=1)
    last = jnp.where(last < 0, slots, last)

    wet = ocean_mask.reshape(tiles, tile_cells)
    return exchange(bands, cap, src, prev, last, partial, covered, wet)


def solution(mesh):
    in_specs = (
        P(None, ("band", "sub")),
        P(("band", "sub"), None, None),
        P(("band", "sub")),
        P(("band", "sub"), None),
        P(("band", "sub")),
        P(("band", "sub")),
    )
    out_specs = P(None, ("band", "sub"))
    return jax.shard_map(
        per_device, mesh=mesh, in_specs=in_specs, out_specs=out_specs, check_vma=False
    )
```

time: 166 us -> 151 us (0.910)
  the two profiles are of different devices: /device:TPU:13 before, /device:TPU:0 now
where the time goes in v2:
time: 151 us; the launch traced here: 149 us
  Pallas kernels  137 us (91%)
  local copies, waits for them, and re-layouts  7.62 us (5%)
  other arithmetic  3.91 us (3%)
    pallas_call x1, Pallas kernels, exchange(): pl.pallas_call(functools.partial(exchange_kernel, bands, cap, chunks, til...  123 us
    pallas_call x1, Pallas kernels, block_products(): pl.pallas_call(functools.partial(block_kernel, group, chunks, bands), gri...  14.1 us
    unnamed x1, local copies, waits for them, and re-layouts  6.12 us

profile of v2, /device:TPU:0, one launch (start us, length us, event | category | flops | bytes accessed | tf_op | source)
XLA Modules:
  0.0 149.0 jit_solution(7864735664333541275)
XLA Ops:
  0.0 0.9 convert_reduce_fusion
  0.9 0.7 multiply_add_fusion
  1.6 0.7 select_reduce_fusion.2
  2.3 0.1 sub.10
  2.4 0.6 pad.4.t_ref
  3.0 14.1 %block_products.1 = (bf16[8,128,8,128]{3,2,1,0:T(8,128)(2,1)}, f32[128,128]{1,0:T(8,128)}, s32[16,1,128]{2,1,0:T(1,128)}) custom-call(bf16[64,16384]{1,0:T(8,128)(2,1)} %v_ref.1, bf16[128,128,128]{2,1,0:T(8,128)(2,1)} %w_ref.1, s32[1,16384]{1,0:T(1,128)} %bitcast.5, s32[16,1,128]{2,1,0:T(1,128)} %pad.4.t_ref), custom_call_target="tpu_custom_call" | custom-call | tf_op jit(solution)/shard_map/block_products/pallas_call | solution.py:88
  17.2 0.7 slice_reduce_fusion
  17.9 0.1 eq.60
  18.0 0.2 select_reduce_fusion
  18.2 0.2 select_reduce_fusion.1
  18.4 0.6 compare_select_fusion.1.prev_ref
  19.0 0.6 compare_select_fusion.last_ref
  19.6 123.3 %exchange.1 = f32[64,25600]{1,0:T(8,128)} custom-call(s32[256]{0:T(256)} %get-tuple-element.12.src_ref, s32[256]{0:T(256)} %compare_select_fusion.1.prev_ref, s32[400]{0:T(512)} %compare_select_fusion.last_ref, bf16[8,128,8,128]{3,2,1,0:T(8,128)(2,1)} %get-tuple-element.9.p_ref, f32[128,128]{1,0:T(8,128)} %get-tuple-element.10.c_ref, s32[200,128]{1,0:T(8,128)} %bitcast.4), custom_call_target="tpu_custom_call" | custom-call | tf_op jit(solution)/shard_map/exchange/pallas_call | solution.py:292
  142.9 6.1 %copy.8 = f32[64,25600]{1,0:T(8,128)} copy(f32[64,25600]{1,0:T(8,128)} %exchange.1) | data formatting | bytes 13107200
  (2 shorter events, 0.0 us)
